TPU v7x, 32 devices: a whole 2x2x4 slice. The times are simulated.
32 devices in a mesh: seq: 8 (over z, y), frame: 4 (over x, core).
Axes of the slice: x: 2, y: 2, z: 4, core: 2. Of those that a mesh axis runs over, the one named last changes fastest.
Arguments:
- patches: bfloat16 [3072, 1280], P('frame'), may hold values from -4 to 4
- vit_gain: float32 [1280], replicated, may hold values from 0.5 to 1.5
- vision_qkv: bfloat16 [1280, 3840], P(None, 'seq')
- vision_out: bfloat16 [1280, 1280], P('seq'), may hold values from -0.15625 to 0.15625
- video_ids: int32 [768], replicated, may hold values from 0 to 2, never falling along the last dimension, each value on 1 to 480 neighbouring positions
- merge_gain: float32 [1280], replicated, may hold values from 0.5 to 1.5
- merge_up: bfloat16 [5120, 5120], P(None, 'seq'), may hold values from -0.078125 to 0.078125
- merge_down: bfloat16 [5120, 8192], P('seq')
- vision_pos: int32 [768], replicated, may hold values from 0 to 4095, as said below
- text_embed: bfloat16 [4096, 8192], P(('seq', 'frame')), may hold values from -6 to 6
- llm_gain: float32 [8192], replicated, may hold values from 0.5 to 1.5
- query_weight: bfloat16 [8192, 2048], P(None, 'frame')
- keyvalue_weight: bfloat16 [8192, 1024], P(None, 'frame')
Outputs:
- context: bfloat16 [4096, 2048], P('seq', 'frame')
Inputs may be any that keep to these rules, and one draw needn't show every extreme that they name: `vision_pos`: distinct positions. Of the tokens in rows f * 192 to (f + 1) * 192 - 1, for any f, at most 36 lie in one block of 512 positions that starts at a multiple of 512; some block holds exactly 36 of them for every f. `video_ids`: the tokens of one video are consecutive rows.
All inputs are finite; a program needn't handle non-finite values.
Results may differ from a plain program's by a relative error of at most 0.02.
Values may be sent and summed in bfloat16 or wider, within the bound.
A program may use at most 128 MiB of HBM per device.

v0:
```python
import math

import jax
import jax.numpy as jnp
from jax import lax
from jax.sharding import PartitionSpec as P

VIT_HDIM = 80
HDIM = 128


epsilon = 1e-06
rope_base = 1000000.0
lowest = -1e30
key_block = 1024


def rms_scale(matrix, scales):
    widened = matrix.astype(jnp.float32)
    factor = lax.rsqrt(jnp.mean(widened * widened, axis=-1, keepdims=True) + epsilon)
    return widened * factor * scales


def rotary(tensor, positions):
    head_width = tensor.shape[-1]
    half_width = head_width // 2
    inverse = rope_base ** (-2.0 * jnp.arange(half_width, dtype=jnp.float32) / head_width)
    angles = positions.astype(jnp.float32)[:, None] * inverse[None, :]
    cosine = jnp.cos(angles)[:, None, :]
    sine_part = jnp.sin(angles)[:, None, :]
    first_half = tensor[..., :half_width]
    second_half = tensor[..., half_width:]
    return jnp.concatenate(
        [
            first_half * cosine - second_half * sine_part,
            second_half * cosine + first_half * sine_part,
        ],
        axis=-1,
    )


def attend_piece(state_now, queries, key_rows, value_rows, allowed, score_scale):
    running_max, running_sum, weighted = state_now
    scores = (
        jnp.einsum("qhgd,khd->hgqk", queries, key_rows, preferred_element_type=jnp.float32)
        * score_scale
    )
    scores = jnp.where(allowed[None, None], scores, lowest)
    new_max = jnp.maximum(running_max, jnp.max(scores, axis=-1))
    weights = jnp.where(allowed[None, None], jnp.exp(scores - new_max[..., None]), 0.0)
    shrink = jnp.exp(running_max - new_max)
    running_sum = running_sum * shrink + jnp.sum(weights, axis=-1)
    update = jnp.einsum(
        "hgqk,khd->qhgd",
        weights.astype(jnp.bfloat16),
        value_rows,
        preferred_element_type=jnp.float32,
    )
    weighted = weighted * jnp.transpose(shrink, (2, 0, 1))[..., None] + update
    return (new_max, running_sum, weighted)


def fold_blocks(state_now, queries, key_rows, value_rows, mask_rule, score_scale, live_rule):
    row_total = key_rows.shape[0]
    step_rows = math.gcd(row_total, key_block)

    def one_block(block_index, state_in):
        offset = block_index * step_rows
        key_part = lax.dynamic_slice_in_dim(key_rows, offset, step_rows, 0)
        value_part = lax.dynamic_slice_in_dim(value_rows, offset, step_rows, 0)

        def attend(state_arg):
            return attend_piece(
                state_arg, queries, key_part, value_part, mask_rule(offset, step_rows), score_scale
            )

        if live_rule is None:
            return attend(state_in)
        return lax.cond(live_rule(offset), attend, lambda state_arg: state_arg, state_in)

    return lax.fori_loop(0, row_total // step_rows, one_block, state_now)


def finish(state_now, row_count):
    running_max, running_sum, weighted = state_now
    mixed = weighted / jnp.transpose(running_sum, (2, 0, 1))[..., None]
    return mixed.reshape(row_count, -1).astype(jnp.bfloat16)


def empty_state(query_rows, head_count, group_count, head_width):
    return (
        jnp.full((head_count, group_count, query_rows), lowest, jnp.float32),
        jnp.zeros((head_count, group_count, query_rows), jnp.float32),
        jnp.zeros((query_rows, head_count, group_count, head_width), jnp.float32),
    )


def local(
    patches,
    vit_gain,
    vision_qkv,
    vision_out,
    video_ids,
    merge_gain,
    merge_up,
    merge_down,
    vision_pos,
    text_embed,
    llm_gain,
    query_weight,
    keyvalue_weight,
):
    frame_index = lax.axis_index("frame")
    seq_index = lax.axis_index("seq")
    frame_count = lax.axis_size("frame")
    seq_count = lax.axis_size("seq")
    patch_rows = patches.shape[0]
    local_heads = vision_qkv.shape[1] // (3 * VIT_HDIM)
    normed_patches = rms_scale(patches, vit_gain).astype(jnp.bfloat16)
    projected = jnp.dot(normed_patches, vision_qkv, preferred_element_type=jnp.float32).astype(
        jnp.bfloat16
    )
    projected = projected.reshape(patch_rows, local_heads, 3, VIT_HDIM)
    vit_query = projected[:, :, 0][:, :, None, :]
    vit_key_rows = projected[:, :, 1]
    vit_value_rows = projected[:, :, 2]
    patch_video = jnp.repeat(video_ids, 4)
    own_video = lax.dynamic_slice_in_dim(patch_video, frame_index * patch_rows, patch_rows)

    def video_mask(key_start, row_count):
        other_video = lax.dynamic_slice_in_dim(patch_video, key_start, row_count)
        return own_video[:, None] == other_video[None, :]

    piece = (
        lax.all_gather(vit_key_rows, "frame", axis=0, tiled=True),
        lax.all_gather(vit_value_rows, "frame", axis=0, tiled=True),
    )
    vit_state = fold_blocks(
        empty_state(patch_rows, local_heads, 1, VIT_HDIM),
        vit_query,
        piece[0],
        piece[1],
        video_mask,
        VIT_HDIM ** (-0.5),
        None,
    )
    vit_context = finish(vit_state, patch_rows)
    head_terms = jnp.dot(vit_context, vision_out, preferred_element_type=jnp.float32)
    head_total = lax.psum(head_terms.astype(jnp.bfloat16), "seq").astype(jnp.float32)
    vit_output = patches.astype(jnp.float32) + head_total
    merged_input = (
        rms_scale(vit_output, merge_gain).astype(jnp.bfloat16).reshape(patch_rows // 4, -1)
    )
    merge_hidden = jax.nn.gelu(
        jnp.dot(merged_input, merge_up, preferred_element_type=jnp.float32), approximate=False
    ).astype(jnp.bfloat16)
    vis_total = vision_pos.shape[0]
    vis_local = vis_total // frame_count
    seq_block = text_embed.shape[0] * frame_count
    capacity = 3 * vis_local // (2 * seq_count)
    token_owner = vision_pos // seq_block
    source = jnp.arange(vis_total, dtype=jnp.int32) // vis_local
    owner_group = source * seq_count + token_owner
    member = (
        owner_group[:, None] == jnp.arange(frame_count * seq_count, dtype=jnp.int32)[None, :]
    ).astype(jnp.int32)
    slot_rank = jnp.sum(member * (jnp.cumsum(member, axis=0) - member), axis=1)
    local_owner = lax.dynamic_slice_in_dim(token_owner, frame_index * vis_local, vis_local)
    local_rank = lax.dynamic_slice_in_dim(slot_rank, frame_index * vis_local, vis_local)
    slot_index = jnp.arange(frame_count * capacity, dtype=jnp.int32)
    matched = (
        (source[None, :] == (slot_index // capacity)[:, None])
        & (token_owner[None, :] == seq_index)
        & (slot_rank[None, :] == (slot_index % capacity)[:, None])
    )
    target = (
        jnp.sum(jnp.where(matched, vision_pos[None, :] - seq_index * seq_block + 1, 0), axis=1) - 1
    )
    target = jnp.where(target < 0, seq_block, target)
    destination = local_owner * capacity + local_rank
    wanted = jnp.arange(capacity * lax.axis_size("seq"), dtype=jnp.int32)
    selector = (destination[None, :] == wanted[:, None]).astype(jnp.bfloat16)
    chosen = jnp.dot(selector, merge_hidden, preferred_element_type=jnp.float32).astype(
        jnp.bfloat16
    )
    vision_rows = lax.psum_scatter(
        jnp.dot(chosen, merge_down, preferred_element_type=jnp.float32).astype(jnp.bfloat16),
        "seq",
        scatter_dimension=0,
        tiled=True,
    )
    text_block, arrived = (
        lax.all_gather(text_embed, "frame", axis=0, tiled=True),
        lax.all_gather(vision_rows, "frame", axis=0, tiled=True),
    )
    embedded = text_block.at[target].set(arrived, mode="drop")
    normed_tokens = rms_scale(embedded, llm_gain).astype(jnp.bfloat16)
    positions = seq_index * seq_block + jnp.arange(seq_block, dtype=jnp.int32)
    group_heads = query_weight.shape[1] // HDIM
    query_full = jnp.dot(normed_tokens, query_weight, preferred_element_type=jnp.float32).reshape(
        seq_block, group_heads, HDIM
    )
    llm_query = (
        rotary(query_full, positions).astype(jnp.bfloat16).reshape(seq_block, 1, group_heads, HDIM)
    )
    pair_full = jnp.dot(normed_tokens, keyvalue_weight, preferred_element_type=jnp.float32).reshape(
        seq_block, 2, HDIM
    )
    llm_key_rows = rotary(pair_full[:, 0:1], positions).astype(jnp.bfloat16)
    llm_value_rows = pair_full[:, 1:2].astype(jnp.bfloat16)
    last_position = positions[seq_block - 1]

    def causal_mask(key_start, row_count):
        return positions[:, None] >= (key_start + jnp.arange(row_count, dtype=jnp.int32))[None, :]

    def causal_live(key_start):
        return key_start <= last_position

    piece = (
        lax.all_gather(llm_key_rows, "seq", axis=0, tiled=True),
        lax.all_gather(llm_value_rows, "seq", axis=0, tiled=True),
    )
    llm_state = fold_blocks(
        empty_state(seq_block, 1, group_heads, HDIM),
        llm_query,
        piece[0],
        piece[1],
        causal_mask,
        HDIM ** (-0.5),
        causal_live,
    )
    return finish(llm_state, seq_block)


def solution(mesh):
    return jax.shard_map(
        local,
        mesh=mesh,
        in_specs=(
            P("frame", None),
            P(),
            P(None, "seq"),
            P("seq", None),
            P(),
            P(),
            P(None, "seq"),
            P("seq", None),
            P(),
            P(("seq", "frame"), None),
            P(),
            P(None, "frame"),
            P(None, "frame"),
        ),
        out_specs=P("seq", "frame"),
        check_vma=False,
    )
```

profile of v0, /device:TPU:24, one launch (start us, length us, event | category | flops | bytes accessed | tf_op | source)
XLA Modules:
  0.0 552.3 jit_solution(12888229057318921247)
XLA Ops:
  12.6 9.7 %all-gather = bf16[3072,2,1,80]{0,3,1,2:T(8,128)(2,1)S(1)} all-gather(bf16[768,2,1,80]{0,3,1,2:T(8,128)(2,1)S(1)} %get-tuple-element.577), channel_id=2, replica_groups=mesh['seq'=8,'frame'=4] {'frame'}, dimensions={0}, use_global_device_ids=true | all-gather | bytes 1228800 | tf_op jit(solution)/shard_map/all_gather | solution.py:135
  22.2 9.8 %all-gather.1 = bf16[3072,2,1,80]{0,3,1,2:T(8,128)(2,1)S(1)} all-gather(bf16[768,2,1,80]{0,3,1,2:T(8,128)(2,1)S(1)} %get-tuple-element.575), channel_id=3, replica_groups=mesh['seq'=8,'frame'=4] {'frame'}, dimensions={0}, use_global_device_ids=true | all-gather | bytes 1228800 | tf_op jit(solution)/shard_map/all_gather | solution.py:136
  32.1 36.5 %while.37 = (s32[]{:T(128)}, f32[2,1,768]{2,0,1:T(2,128)S(1)}, f32[2,1,768]{2,0,1:T(2,128)S(1)}, f32[768,2,1,80]{0,3,1,2:T(8,128)}, s32[768]{0:T(1024)S(1)}, /*i...) while((s32[]{:T(128)}, f32[2,1,768]{2,0,1:T(2,128)S(1)}, ...), condition=%wide.region_8.9_spmd.clone, body=%wide.region_5.8_spmd.clone.sunk | while | flops 524928000 | bytes 49183964 | solution.py:81
  32.6 4.1 fusion.243
  36.8 5.7 %fusion.246 = f32[768,2,1,80]{0,3,1,2:T(8,128)} fusion(f32[2,1024,768]{2,1,0:T(8,128)} %get-tuple-element.712, f32[2,768]{1,0:T(2,128)S(1)} %bitcast.185, pred[768,1024]{0,1:T(8,128)(4,1)S(1)} %broadcast_compare_fusion.4, f32[768,2,1,80]{0,3,1,2:T(8,128)} %get-tuple-element.736, bf16[3072,2,80]{0,2,1:T(8,128)(2,1)S(1)} %get-tuple-element.754, ...), kind=kOutput, calls=%fused_computation.40.clone.1 | convolution fusion | flops 259891200 | bytes 8400901 | tf_op jit(solution)/shard_map/while/body/eval_jaxpr/hgqk,khd->qhgd/dot_general | solution.py:53
  44.7 4.1 fusion.243
  48.9 5.8 %fusion.246 = f32[768,2,1,80]{0,3,1,2:T(8,128)} fusion(f32[2,1024,768]{2,1,0:T(8,128)} %get-tuple-element.712, f32[2,768]{1,0:T(2,128)S(1)} %bitcast.185, pred[768,1024]{0,1:T(8,128)(4,1)S(1)} %broadcast_compare_fusion.4, f32[768,2,1,80]{0,3,1,2:T(8,128)} %get-tuple-element.736, bf16[3072,2,80]{0,2,1:T(8,128)(2,1)S(1)} %get-tuple-element.754, ...), kind=kOutput, calls=%fused_computation.40.clone.1 | convolution fusion | flops 259891200 | bytes 8400901 | tf_op jit(solution)/shard_map/while/body/eval_jaxpr/hgqk,khd->qhgd/dot_general | solution.py:53
  56.9 4.1 fusion.243
  61.1 5.8 %fusion.246 = f32[768,2,1,80]{0,3,1,2:T(8,128)} fusion(f32[2,1024,768]{2,1,0:T(8,128)} %get-tuple-element.712, f32[2,768]{1,0:T(2,128)S(1)} %bitcast.185, pred[768,1024]{0,1:T(8,128)(4,1)S(1)} %broadcast_compare_fusion.4, f32[768,2,1,80]{0,3,1,2:T(8,128)} %get-tuple-element.736, bf16[3072,2,80]{0,2,1:T(8,128)(2,1)S(1)} %get-tuple-element.754, ...), kind=kOutput, calls=%fused_computation.40.clone.1 | convolution fusion | flops 259891200 | bytes 8400901 | tf_op jit(solution)/shard_map/while/body/eval_jaxpr/hgqk,khd->qhgd/dot_general | solution.py:53
  74.4 95.3 %all-reduce.4.cloned.1.call-done = bf16[768,1280]{1,0:T(8,128)(2,1)} async-done(((bf16[768,1280]{1,0:T(8,128)(2,1)}), bf16[768,1280]{1,0:T(8,128)(2,1)}) %all-reduce.4.cloned.1.call-update) | async-done | bytes 1966096 | tf_op jit(solution)/shard_map/psum | solution.py:149
  178.5 4.6 fusion.226
  183.0 10.2 %convolution_convert_fusion = bf16[288,8192]{1,0:T(8,128)(2,1)} fusion(bf16[640,8192]{1,0:T(8,128)(2,1)} %param.26, f32[192,640]{1,0:T(8,128)S(1)} %fusion.226, s32[192]{0:T(256)S(1)} %dynamic-slice_add_fusion), kind=kOutput, calls=%fused_computation.62 | convolution fusion | flops 3101263872 | bytes 15696640 | tf_op jit(solution)/shard_map/dot_general | solution.py:187
  193.3 108.4 %fusion.2 = bf16[40,8192]{1,0:T(8,128)(2,1)S(1)} fusion(bf16[288,8192]{1,0:T(8,128)(2,1)} %convolution_convert_fusion), kind=kCustom, calls=%all-reduce-scatter | all-reduce-scatter fusion | flops 2621441 | bytes 5374464
  301.8 4.3 collective-permute-start
  307.3 10.5 %collective-permute-done = bf16[28,8192]{1,0:T(8,128)(2,1)S(1)} collective-permute-done((bf16[28,8192]{1,0:T(8,128)(2,1)S(1)}, bf16[28,8192]{1,0:T(8,128)(2,1)S(1)}, u32[]{:S(2)}, u32[]{:S(2)}) %collective-permute-start) | collective-permute-done | bytes 458784
  321.2 25.2 %all-gather.14.cloned.1.call-done = bf16[4,36,8192]{2,1,0:T(8,128)(2,1)} async-done(((bf16[1,36,8192]{2,1,0:T(8,128)(2,1)}), bf16[4,36,8192]{2,1,0:T(8,128)(2,1)}) %all-gather.14.cloned.1.call-update) | async-done | bytes 2359312 | tf_op jit(solution)/shard_map/all_gather | solution.py:194
  349.5 56.8 %all-gather.8.cloned.1.call-done = bf16[512,8192]{1,0:T(8,128)(2,1)} async-done(((bf16[128,8192]{1,0:T(8,128)(2,1)}), bf16[512,8192]{1,0:T(8,128)(2,1)}) %all-gather.8.cloned.1.call-update) | async-done | bytes 8388624 | tf_op jit(solution)/shard_map/all_gather | solution.py:193
  406.3 13.2 %scatter_fusion = bf16[512,8192]{1,0:T(8,128)(2,1)} fusion(bf16[512,8192]{1,0:T(8,128)(2,1)} %all-gather.8.cloned.1.call-done, s32[144]{0:T(256)S(1)} %bitcast.198, bf16[144,8192]{1,0:T(8,128)(2,1)} %reshape.464), kind=kCustom, calls=%fused_computation | custom fusion | bytes 7078464 | tf_op jit(solution)/shard_map/scatter | solution.py:196
  419.5 5.3 fusion.51
  425.3 5.1 fusion.59
  433.9 11.6 %fusion.57 = f32[512,512]{0,1:T(8,128)S(1)} fusion(bf16[8192,512]{1,0:T(8,128)(2,1)} %param.30, bf16[512,8192]{1,0:T(8,128)(2,1)} %scatter_fusion, f32[8192]{0:T(1024)S(1)} %copy-done.9, f32[512]{0:T(512)S(1)} %add_rsqrt_fusion.2), kind=kOutput, calls=%fused_computation.72 | convolution fusion | flops 4311744512 | bytes 17860608 | tf_op jit(solution)/shard_map/dot_general | solution.py:200
  446.9 22.7 %all-gather.10.cloned.1.call-done = bf16[4096,1,128]{0,2,1:T(8,128)(2,1)} async-done(((bf16[512,1,128]{0,2,1:T(8,128)(2,1)}), bf16[4096,1,128]{0,2,1:T(8,128)(2,1)}) %all-gather.10.cloned.1.call-update) | async-done | bytes 1048592 | tf_op jit(solution)/shard_map/all_gather | solution.py:220
  471.2 38.7 %all-gather.12.cloned.1.call-done = bf16[4096,1,128]{0,2,1:T(8,128)(2,1)} async-done(((bf16[512,1,128]{0,2,1:T(8,128)(2,1)}), bf16[4096,1,128]{0,2,1:T(8,128)(2,1)}) %all-gather.12.cloned.1.call-update) | async-done | bytes 1048592 | tf_op jit(solution)/shard_map/all_gather | solution.py:221
  510.1 33.9 %while.36 = (s32[]{:T(128)}, f32[1,4,512]{2,1,0:T(4,128)S(1)}, f32[1,4,512]{2,1,0:T(4,128)S(1)}, f32[512,1,4,128]{0,3,2,1:T(8,128)S(1)}, s32[]{:T(128)}, /*index...) while((s32[]{:T(128)}, f32[1,4,512]{2,1,0:T(4,128)S(1)}, ...), condition=%wide.region_19.20_spmd.clone, body=%wide.region_14.19_spmd.clone.sunk | while | flops 1102061056 | bytes 30556472 | solution.py:81
  510.7 7.9 %conditional.3 = ((f32[1,4,512]{2,1,0:T(4,128)S(1)}, f32[1,4,512]{2,1,0:T(4,128)S(1)}, f32[512,1,4,128]{0,3,2,1:T(8,128)S(1)})) conditional(s32[]{:T(128)} %convert_element_type.191, (f32[1,4,512]{2,1,0:T(4,128)S(1)}, f32[1,4,512]{2,1,0:T(4,128)S(1)}, f32[512,1,4,128]{0,3,2,1:T(8,128)S(1)}) %tuple.98, (s32[]{:T(128)}, s32[]{:T(128)}, ...), branch_computations={%region_15.15_spmd, %region_16.18_spmd} | conditional | flops 1102061056 | bytes 30554194 | solution.py:79
  512.7 3.7 fusion.13
  519.1 7.9 %conditional.3 = ((f32[1,4,512]{2,1,0:T(4,128)S(1)}, f32[1,4,512]{2,1,0:T(4,128)S(1)}, f32[512,1,4,128]{0,3,2,1:T(8,128)S(1)})) conditional(s32[]{:T(128)} %convert_element_type.191, (f32[1,4,512]{2,1,0:T(4,128)S(1)}, f32[1,4,512]{2,1,0:T(4,128)S(1)}, f32[512,1,4,128]{0,3,2,1:T(8,128)S(1)}) %tuple.98, (s32[]{:T(128)}, s32[]{:T(128)}, ...), branch_computations={%region_15.15_spmd, %region_16.18_spmd} | conditional | flops 1102061056 | bytes 30554194 | solution.py:79
  521.1 3.7 fusion.13
  527.6 7.9 %conditional.3 = ((f32[1,4,512]{2,1,0:T(4,128)S(1)}, f32[1,4,512]{2,1,0:T(4,128)S(1)}, f32[512,1,4,128]{0,3,2,1:T(8,128)S(1)})) conditional(s32[]{:T(128)} %convert_element_type.191, (f32[1,4,512]{2,1,0:T(4,128)S(1)}, f32[1,4,512]{2,1,0:T(4,128)S(1)}, f32[512,1,4,128]{0,3,2,1:T(8,128)S(1)}) %tuple.98, (s32[]{:T(128)}, s32[]{:T(128)}, ...), branch_computations={%region_15.15_spmd, %region_16.18_spmd} | conditional | flops 1102061056 | bytes 30554194 | solution.py:79
  529.6 3.7 fusion.13
  536.1 7.9 %conditional.3 = ((f32[1,4,512]{2,1,0:T(4,128)S(1)}, f32[1,4,512]{2,1,0:T(4,128)S(1)}, f32[512,1,4,128]{0,3,2,1:T(8,128)S(1)})) conditional(s32[]{:T(128)} %convert_element_type.191, (f32[1,4,512]{2,1,0:T(4,128)S(1)}, f32[1,4,512]{2,1,0:T(4,128)S(1)}, f32[512,1,4,128]{0,3,2,1:T(8,128)S(1)}) %tuple.98, (s32[]{:T(128)}, s32[]{:T(128)}, ...), branch_computations={%region_15.15_spmd, %region_16.18_spmd} | conditional | flops 1102061056 | bytes 30554194 | solution.py:79
  538.1 3.7 fusion.13
  (141 shorter events, 59.0 us)
Async XLA Ops:
  6.5 3.2 copy-start
  6.5 163.1 %all-reduce.4.cloned.1.call-start = ((), (), s32[]{:S(2)}) async-start(), calls=%async_computation.1 | async-start | bytes 3932160 | tf_op jit(solution)/shard_map/psum | solution.py:149
  32.1 37.7 %copy-start.5 = (bf16[160,1280]{1,0:T(8,128)(2,1)S(1)}, bf16[160,1280]{1,0:T(8,128)(2,1)}, u32[]{:S(2)}) copy-start(bf16[160,1280]{1,0:T(8,128)(2,1)} %param.22) | copy-start | bytes 1228804
  32.1 40.0 %copy-start.6 = (s32[768]{0:T(1024)S(1)}, s32[768]{0:T(1024)}, u32[]{:S(2)}) copy-start(s32[768]{0:T(1024)} %param.27) | copy-start | bytes 9220
  36.8 5.7 %copy-start.2 = (f32[2,1024,768]{2,1,0:T(8,128)S(1)}, f32[2,1024,768]{2,1,0:T(8,128)}, u32[]{:S(2)}) copy-start(f32[2,1024,768]{2,1,0:T(8,128)} %get-tuple-element.712) | copy-start | bytes 18874372 | tf_op jit(solution)/shard_map/while
  48.9 5.8 %copy-start.2 = (f32[2,1024,768]{2,1,0:T(8,128)S(1)}, f32[2,1024,768]{2,1,0:T(8,128)}, u32[]{:S(2)}) copy-start(f32[2,1024,768]{2,1,0:T(8,128)} %get-tuple-element.712) | copy-start | bytes 18874372 | tf_op jit(solution)/shard_map/while
  61.1 5.8 %copy-start.2 = (f32[2,1024,768]{2,1,0:T(8,128)S(1)}, f32[2,1024,768]{2,1,0:T(8,128)}, u32[]{:S(2)}) copy-start(f32[2,1024,768]{2,1,0:T(8,128)} %get-tuple-element.712) | copy-start | bytes 18874372 | tf_op jit(solution)/shard_map/while
  68.6 101.1 %copy-start.4 = (bf16[768,1280]{1,0:T(8,128)(2,1)S(1)}, bf16[768,1280]{1,0:T(8,128)(2,1)}, u32[]{:S(2)}) copy-start(bf16[768,1280]{1,0:T(8,128)(2,1)} %param.19) | copy-start | bytes 5898244
  68.6 103.3 %copy-start.7 = (f32[1280]{0:T(1024)S(1)}, f32[1280]{0:T(1024)}, u32[]{:S(2)}) copy-start(f32[1280]{0:T(1024)} %param.24) | copy-start | bytes 15364
  71.9 274.6 %all-gather.14.cloned.1.call-start = ((), (), s32[]{:S(2)}) async-start(), calls=%async_computation.4 | async-start | bytes 3276800 | tf_op jit(solution)/shard_map/all_gather | solution.py:194
  193.3 112.8 %copy-start.8 = (u32[32]{0:T(128)S(1)}, u32[32]{0:T(128)}, u32[]{:S(2)}) copy-start(u32[32]{0:T(128)} %constant.264) | copy-start | bytes 388
  301.8 16.1 %collective-permute-start = (bf16[28,8192]{1,0:T(8,128)(2,1)S(1)}, bf16[28,8192]{1,0:T(8,128)(2,1)S(1)}, u32[]{:S(2)}, u32[]{:S(2)}) collective-permute-start(bf16[28,8192]{1,0:T(8,128)(2,1)S(1)} %slice.57), channel_id=1, source_target_pairs={{0,4},{4,8},{8,12},{12,16},{16,20},{20,24},{24,28},{1,5},{5,9},{9,... | collective-permute-start | bytes 1376264
  319.8 86.5 %all-gather.8.cloned.1.call-start = ((), (), s32[]{:S(2)}) async-start(), calls=%async_computation | async-start | bytes 10485760 | tf_op jit(solution)/shard_map/all_gather | solution.py:193
  320.6 149.0 %all-gather.10.cloned.1.call-start = ((), (), s32[]{:S(2)}) async-start(), calls=%async_computation.2 | async-start | bytes 1179648 | tf_op jit(solution)/shard_map/all_gather | solution.py:220
  406.3 18.5 %copy-start.9 = (f32[8192]{0:T(1024)S(1)}, f32[8192]{0:T(1024)}, u32[]{:S(2)}) copy-start(f32[8192]{0:T(1024)} %param.29) | copy-start | bytes 98308
  419.5 5.8 %copy-start.3 = (bf16[512,8192]{1,0:T(8,128)(2,1)S(1)}, bf16[512,8192]{1,0:T(8,128)(2,1)}, u32[]{:S(2)}) copy-start(bf16[512,8192]{1,0:T(8,128)(2,1)} %scatter_fusion) | copy-start | bytes 25165828
  431.6 78.3 %all-gather.12.cloned.1.call-start = ((), (), s32[]{:S(2)}) async-start(), calls=%async_computation.3 | async-start | bytes 1179648 | tf_op jit(solution)/shard_map/all_gather | solution.py:221
  544.0 1.3 copy-start.1
Sparse Core Ops, SparseCore 0:
  72.0 97.6 all-reduce.3
  319.9 26.4 all-gather.13
  348.0 58.2 all-gather.7
  431.7 37.8 all-gather.9
  471.5 38.3 all-gather.11
where the time goes:
time: 560 us; the launch traced here: 552 us
  waiting for transfers between devices  250 us (45%)
  blocking collectives  128 us (23%)
  matrix products  87.1 us (16%)
  other arithmetic  36.2 us (6%)
  local copies, waits for them, and re-layouts  28.9 us (5%)
  between operations  14.7 us (3%)
    unnamed x1, blocking collectives  108 us
    psum x1, waiting for transfers between devices, local(): lax.psum(head_terms.astype(jnp.bfloat16), 'seq').astype(jnp.float32)  95.3 us
    all_gather x1, waiting for transfers between devices, local(): lax.all_gather(text_embed, 'frame', axis=0, tiled=True)  56.8 us
    all_gather x1, waiting for transfers between devices, local(): lax.all_gather(llm_value_rows, 'seq', axis=0, tiled=True)  38.7 us
    dot_general x7, matrix products, attend_piece(): jnp.einsum('hgqk,khd->qhgd', weights.astype(jnp.bfloat16), value_rows, pr...  32.1 us
    all_gather x1, waiting for transfers between devices, local(): lax.all_gather(vision_rows, 'frame', axis=0, tiled=True)  25.2 us
    all_gather x1, waiting for transfers between devices, local(): lax.all_gather(llm_key_rows, 'seq', axis=0, tiled=True)  22.7 us
    dot_general x7, matrix products, attend_piece(): jnp.einsum('qhgd,khd->hgqk', queries, key_rows, preferred_element_type=jn...  18.7 us
  transfers between devices with their start and end apart: 6, of which 6 were waited for; matrix products, arithmetic and copies ran while one was open for 4% of the time, Pallas kernels for 0%

commit v1 on v0

v1 whole, which is shorter than its diff:
```python
import math

import jax
import jax.numpy as jnp
from jax import lax
from jax.experimental import pallas as pl
from jax.experimental.pallas import tpu as pltpu
from jax.sharding import PartitionSpec as P

VIT_HDIM = 80
HDIM = 128


epsilon = 1e-06
rope_base = 1000000.0
lowest = -1e30
vmem_limit = 56 * 1024 * 1024


def rms_scale(matrix, scales):
    widened = matrix.astype(jnp.float32)
    factor = lax.rsqrt(jnp.mean(widened * widened, axis=-1, keepdims=True) + epsilon)
    return widened * factor * scales


def rotary(tensor, positions):
    head_width = tensor.shape[-1]
    half_width = head_width // 2
    inverse = rope_base ** (-2.0 * jnp.arange(half_width, dtype=jnp.float32) / head_width)
    angles = positions.astype(jnp.float32)[:, None] * inverse[None, :]
    cosine = jnp.cos(angles)[:, None, :]
    sine_part = jnp.sin(angles)[:, None, :]
    first_half = tensor[..., :half_width]
    second_half = tensor[..., half_width:]
    return jnp.concatenate(
        [
            first_half * cosine - second_half * sine_part,
            second_half * cosine + first_half * sine_part,
        ],
        axis=-1,
    )


def vit_attention_kernel(own_ref, ids_ref, q_ref, k_ref, v_ref, out_ref):
    allowed = own_ref[...] == ids_ref[...]
    parts = []
    for head in range(q_ref.shape[1] // VIT_HDIM):
        columns = slice(head * VIT_HDIM, (head + 1) * VIT_HDIM)
        scores = lax.dot_general(
            q_ref[:, columns],
            k_ref[:, columns],
            (((1,), (1,)), ((), ())),
            preferred_element_type=jnp.float32,
        )
        scores = jnp.where(allowed, scores, lowest)
        highest = jnp.max(scores, axis=1, keepdims=True)
        weights = jnp.exp((scores - highest) * VIT_HDIM ** (-0.5))
        row_sum = jnp.sum(weights, axis=1, keepdims=True)
        mixed = jnp.dot(
            weights.astype(jnp.bfloat16), v_ref[:, columns], preferred_element_type=jnp.float32
        )
        parts.append(mixed / row_sum)
    out_ref[...] = jnp.concatenate(parts, axis=1).astype(out_ref.dtype)


def vit_attention(own_ids, all_ids, queries, key_rows, value_rows):
    rows, width = queries.shape
    keys = key_rows.shape[0]
    step = math.gcd(rows, 256)
    return pl.pallas_call(
        vit_attention_kernel,
        grid=(rows // step,),
        in_specs=[
            pl.BlockSpec((step, 1), lambda i: (i, 0)),
            pl.BlockSpec((1, keys), lambda i: (0, 0)),
            pl.BlockSpec((step, width), lambda i: (i, 0)),
            pl.BlockSpec((keys, width), lambda i: (0, 0)),
            pl.BlockSpec((keys, width), lambda i: (0, 0)),
        ],
        out_specs=pl.BlockSpec((step, width), lambda i: (i, 0)),
        out_shape=jax.ShapeDtypeStruct((rows, width), jnp.bfloat16),
        compiler_params=pltpu.CompilerParams(vmem_limit_bytes=vmem_limit),
    )(own_ids[:, None], all_ids[None, :], queries, key_rows, value_rows)


def causal_kernel(block_ref, q_ref, k_ref, v_ref, out_ref):
    rows = q_ref.shape[0]
    queries = q_ref[...]

    def fold(start, state_in, masked):
        running_max, running_sum, weighted = state_in
        scores = lax.dot_general(
            queries,
            k_ref[pl.ds(start, rows), :],
            (((1,), (1,)), ((), ())),
            preferred_element_type=jnp.float32,
        )
        if masked:
            row_id = lax.broadcasted_iota(jnp.int32, (rows, rows), 0)
            column_id = lax.broadcasted_iota(jnp.int32, (rows, rows), 1)
            scores = jnp.where(row_id >= column_id, scores, lowest)
        new_max = jnp.maximum(running_max, jnp.max(scores, axis=1, keepdims=True))
        weights = jnp.exp((scores - new_max) * HDIM ** (-0.5))
        shrink = jnp.exp((running_max - new_max) * HDIM ** (-0.5))
        running_sum = running_sum * shrink + jnp.sum(weights, axis=1, keepdims=True)
        update = jnp.dot(
            weights.astype(jnp.bfloat16),
            v_ref[pl.ds(start, rows), :],
            preferred_element_type=jnp.float32,
        )
        return (new_max, running_sum, weighted * shrink + update)

    state = (
        jnp.full((rows, 1), lowest, jnp.float32),
        jnp.zeros((rows, 1), jnp.float32),
        jnp.zeros((rows, HDIM), jnp.float32),
    )
    own = block_ref[0]
    state = fold(pl.multiple_of(own * rows, rows), state, True)
    _, running_sum, weighted = lax.fori_loop(
        0, own, lambda i, now: fold(pl.multiple_of(i * rows, rows), now, False), state
    )
    out_ref[...] = (weighted / running_sum).astype(out_ref.dtype)


def causal_attention(block_index, queries, key_rows, value_rows):
    rows, width = queries.shape
    keys = key_rows.shape[0]
    return pl.pallas_call(
        causal_kernel,
        grid=(width // HDIM,),
        in_specs=[
            pl.BlockSpec(memory_space=pltpu.SMEM),
            pl.BlockSpec((rows, HDIM), lambda h: (0, h)),
            pl.BlockSpec((keys, HDIM), lambda h: (0, 0)),
            pl.BlockSpec((keys, HDIM), lambda h: (0, 0)),
        ],
        out_specs=pl.BlockSpec((rows, HDIM), lambda h: (0, h)),
        out_shape=jax.ShapeDtypeStruct((rows, width), jnp.bfloat16),
        compiler_params=pltpu.CompilerParams(vmem_limit_bytes=vmem_limit),
    )(block_index[None], queries, key_rows, value_rows)


def project(tokens, positions, query_weight, keyvalue_weight):
    rows = tokens.shape[0]
    query_full = jnp.dot(tokens, query_weight, preferred_element_type=jnp.float32)
    query = rotary(query_full.reshape(rows, -1, HDIM), positions).reshape(rows, -1)
    pair_full = jnp.dot(tokens, keyvalue_weight, preferred_element_type=jnp.float32)
    key = rotary(pair_full[:, :HDIM].reshape(rows, 1, HDIM), positions).reshape(rows, HDIM)
    pair = jnp.concatenate([key, pair_full[:, HDIM:]], axis=1)
    return query.astype(jnp.bfloat16), pair.astype(jnp.bfloat16)


def place(token_pos, first, text_rows, vision_rows):
    spots = first + jnp.arange(text_rows.shape[0], dtype=jnp.int32)
    hit = spots[:, None] == token_pos[None, :]
    moved = jnp.dot(hit.astype(jnp.bfloat16), vision_rows, preferred_element_type=jnp.float32)
    taken = jnp.any(hit, axis=1, keepdims=True)
    return jnp.where(taken, moved.astype(jnp.bfloat16), text_rows)


def local(
    patches,
    vit_gain,
    vision_qkv,
    vision_out,
    video_ids,
    merge_gain,
    merge_up,
    merge_down,
    vision_pos,
    text_embed,
    llm_gain,
    query_weight,
    keyvalue_weight,
):
    frame_index = lax.axis_index("frame")
    seq_index = lax.axis_index("seq")
    frame_count = lax.axis_size("frame")
    seq_count = lax.axis_size("seq")
    patch_rows = patches.shape[0]
    local_heads = vision_qkv.shape[1] // (3 * VIT_HDIM)
    normed_patches = rms_scale(patches, vit_gain).astype(jnp.bfloat16)
    projected = jnp.dot(normed_patches, vision_qkv, preferred_element_type=jnp.float32).astype(
        jnp.bfloat16
    )
    width = local_heads * VIT_HDIM
    projected = projected.reshape(patch_rows, local_heads, 3, VIT_HDIM)
    vit_query = projected[:, :, 0].reshape(patch_rows, width)
    vit_key = projected[:, :, 1].reshape(patch_rows, width)
    vit_value = projected[:, :, 2].reshape(patch_rows, width)
    patch_video = jnp.repeat(video_ids, 4)
    own_video = lax.dynamic_slice_in_dim(patch_video, frame_index * patch_rows, patch_rows)
    out_full = lax.all_gather(vision_out, "seq", axis=0, tiled=True)
    key_all = lax.all_gather(vit_key, "frame", axis=0, tiled=True)
    value_all = lax.all_gather(vit_value, "frame", axis=0, tiled=True)
    vit_context = vit_attention(own_video, patch_video, vit_query, key_all, value_all)
    context_all = lax.all_gather(vit_context.T, "seq", axis=0, tiled=True)
    head_total = lax.dot_general(
        context_all, out_full, (((0,), (0,)), ((), ())), preferred_element_type=jnp.float32
    )
    vit_output = patches.astype(jnp.float32) + head_total
    merged_input = (
        rms_scale(vit_output, merge_gain).astype(jnp.bfloat16).reshape(patch_rows // 4, -1)
    )
    merge_hidden = jax.nn.gelu(
        jnp.dot(merged_input, merge_up, preferred_element_type=jnp.float32), approximate=False
    ).astype(jnp.bfloat16)

    text_embed, context_tie = lax.optimization_barrier((text_embed, context_all))
    seq_block = text_embed.shape[0] * frame_count
    text_block = lax.all_gather(text_embed, "frame", axis=0, tiled=True)
    text_tokens = rms_scale(text_block, llm_gain).astype(jnp.bfloat16)
    first = seq_index * seq_block
    positions = first + jnp.arange(seq_block, dtype=jnp.int32)
    text_query, text_pair = project(text_tokens, positions, query_weight, keyvalue_weight)
    text_pair_all = lax.all_gather(text_pair, "seq", axis=0, tiled=True)

    vision_rows = lax.psum_scatter(
        jnp.dot(merge_hidden, merge_down, preferred_element_type=jnp.float32).astype(jnp.bfloat16),
        "seq",
        scatter_dimension=0,
        tiled=True,
    )
    share = vision_rows.shape[0]
    token_pos = vision_pos.reshape(frame_count, seq_count, share).transpose(1, 0, 2)
    vision_normed = rms_scale(vision_rows, llm_gain).astype(jnp.bfloat16)
    vision_tokens = lax.all_gather(vision_normed, "frame", axis=0, tiled=True)
    here = lax.dynamic_index_in_dim(token_pos, seq_index, 0, keepdims=False).reshape(-1)
    vision_query, vision_pair = project(vision_tokens, here, query_weight, keyvalue_weight)
    vision_all = lax.all_gather(
        jnp.concatenate([vision_query, vision_pair], axis=1), "seq", axis=0, tiled=True
    )
    token_pos = token_pos.reshape(-1)
    query_width = vision_query.shape[1]
    llm_query = place(token_pos, first, text_query, vision_all[:, :query_width])
    llm_pair = place(token_pos, 0, text_pair_all, vision_all[:, query_width:])
    return causal_attention(seq_index, llm_query, llm_pair[:, :HDIM], llm_pair[:, HDIM:])


def solution(mesh):
    return jax.shard_map(
        local,
        mesh=mesh,
        in_specs=(
            P("frame", None),
            P(),
            P(None, "seq"),
            P("seq", None),
            P(),
            P(),
            P(None, "seq"),
            P("seq", None),
            P(),
            P(("seq", "frame"), None),
            P(),
            P(None, "frame"),
            P(None, "frame"),
        ),
        out_specs=P("seq", "frame"),
        check_vma=False,
    )
```

time: 560 us -> 474 us (0.85)
  blocking collectives: 128 us -> 26.9 us
  waiting for transfers between devices: 250 us -> 312 us
  Pallas kernels: 0 us -> 34.7 us
  matrix products: 87.1 us -> 53.1 us
  other arithmetic: 36.2 us -> 18.5 us
  local copies, waits for them, and re-layouts: 28.9 us -> 11.9 us
    unnamed x1 -> x0, blocking collectives: 108 us -> none
    psum x1 -> x0, waiting for transfers between devices: 95.3 us -> none  [local(): lax.psum(head_terms.astype(jnp.bfloat16), 'seq').astype(jnp.float32)]
    all_gather x4 -> x6, waiting for transfers between devices: 143 us -> 237 us  [the longest x1 62.4 us: local(): out_full = lax.all_gather(vision_out, 'seq', axis=0, tiled=True)]
    reduce_scatter x0 -> x1, waiting for transfers between devices: none -> 72.9 us  [local(): lax.psum_scatter(jnp.dot(merge_hidden, merge_down, preferred_element_type...]
    pallas_call x0 -> x2, Pallas kernels: none -> 34.7 us  [the longest x1 22.3 us: causal_attention(): pl.pallas_call(causal_kernel, grid=(width // HDIM,), in_specs=[pl.BlockSp...]
    dot_general x19 -> x8, matrix products: 84.3 us -> 50.3 us  [the longest x2 16.2 us: project(): jnp.dot(tokens, query_weight, preferred_element_type=jnp.float32)]
    reduce_sum x9 -> x0, other arithmetic: 13.8 us -> none  [the longest x7 13.4 us: attend_piece(): running_sum = running_sum * shrink + jnp.sum(weights, axis=-1)]
    scatter x1 -> x0, local copies, waits for them, and re-layouts: 13.2 us -> none  [local(): embedded = text_block.at[target].set(arrived, mode='drop')]
  transfers between devices with their start and end apart: 6 -> 7, of which waited for: 6 -> 7; matrix products, arithmetic and copies ran while one was open for 4% -> 9% of each run, Pallas kernels for 0% -> 0%
where the time goes in v1:
time: 474 us; the launch traced here: 471 us
  waiting for transfers between devices  312 us (66%)
  matrix products  53.1 us (11%)
  Pallas kernels  34.7 us (7%)
  blocking collectives  26.9 us (6%)
  other arithmetic  18.5 us (4%)
  between operations  13.8 us (3%)
  local copies, waits for them, and re-layouts  11.9 us (3%)
    reduce_scatter x1, waiting for transfers between devices, local(): lax.psum_scatter(jnp.dot(merge_hidden, merge_down, preferred_element_type...  72.9 us
    all_gather x1, waiting for transfers between devices, local(): out_full = lax.all_gather(vision_out, 'seq', axis=0, tiled=True)  62.4 us
    all_gather x1, waiting for transfers between devices, local(): text_block = lax.all_gather(text_embed, 'frame', axis=0, tiled=True)  49.5 us
    all_gather x1, waiting for transfers between devices, local(): text_pair_all = lax.all_gather(text_pair, 'seq', axis=0, tiled=True)  47.2 us
    all_gather x1, waiting for transfers between devices, local(): context_all = lax.all_gather(vit_context.T, 'seq', axis=0, tiled=True)  46.1 us
    pallas_call x1, Pallas kernels, causal_attention(): pl.pallas_call(causal_kernel, grid=(width // HDIM,), in_specs=[pl.BlockSp...  22.3 us
    all_gather x1, waiting for transfers between devices, local(): vision_tokens = lax.all_gather(vision_normed, 'frame', axis=0, tiled=True)  19.4 us
    dot_general x2, matrix products, project(): jnp.dot(tokens, query_weight, preferred_element_type=jnp.float32)  16.2 us
  transfers between devices with their start and end apart: 7, of which 7 were waited for; matrix products, arithmetic and copies ran while one was open for 9% of the time, Pallas kernels for 0%

profile of v1, /device:TPU:24, one launch (start us, length us, event | category | flops | bytes accessed | tf_op | source)
XLA Modules:
  0.0 471.3 jit_solution(15295477310683278825)
XLA Ops:
  6.5 0.9 broadcast_in_dim.18
  9.6 2.0 fusion.8
  11.6 2.8 fusion.21
  14.4 0.9 copy.77.q_ref
  15.5 13.3 %all_gather.24.k_ref = bf16[3072,160]{1,0:T(8,128)(2,1)} all-gather(bf16[768,160]{1,0:T(8,128)(2,1)S(1)} %copy.73), channel_id=1, replica_groups=mesh['seq'=8,'frame'=4] {'frame'}, dimensions={0}, use_global_device_ids=true | all-gather | bytes 1228800 | tf_op jit(solution)/shard_map/all_gather | solution.py:195
  29.0 13.6 %all_gather.25.v_ref = bf16[3072,160]{1,0:T(8,128)(2,1)} all-gather(bf16[768,160]{1,0:T(8,128)(2,1)S(1)} %copy.75), channel_id=1, replica_groups=mesh['seq'=8,'frame'=4] {'frame'}, dimensions={0}, use_global_device_ids=true | all-gather | bytes 1228800 | tf_op jit(solution)/shard_map/all_gather | solution.py:196
  42.6 12.5 %shard_map.127 = bf16[768,160]{1,0:T(8,128)(2,1)} custom-call(s32[768,1]{1,0:T(8,128)} %broadcast_in_dim.21.own_ref, s32[1,3072]{1,0:T(1,128)} %broadcast_in_dim_reshape.2.ids_ref, bf16[768,160]{1,0:T(8,128)(2,1)} %copy.77.q_ref, bf16[3072,160]{1,0:T(8,128)(2,1)} %all_gather.24.k_ref, bf16[3072,160]{1,0:T(8,128)(2,1)} %all_gather.25.v_ref), custom_call_target="tpu_custom_call" | custom-call | tf_op jit(solution)/shard_map/pallas_call | solution.py:70
  55.0 1.8 copy.78
  57.9 46.1 %all-gather.7.cloned.1.call-done = bf16[1280,768]{1,0:T(8,128)(2,1)} async-done(((bf16[160,768]{1,0:T(8,128)(2,1)}), bf16[1280,768]{1,0:T(8,128)(2,1)}) %all-gather.7.cloned.1.call-update) | async-done | bytes 1966096 | tf_op jit(solution)/shard_map/all_gather | solution.py:198
  104.0 62.4 %all-gather.9.cloned.1.call-done = bf16[1280,1280]{1,0:T(8,128)(2,1)} async-done(((bf16[160,1280]{1,0:T(8,128)(2,1)}), bf16[1280,1280]{1,0:T(8,128)(2,1)}) %all-gather.9.cloned.1.call-update) | async-done | bytes 3276816 | tf_op jit(solution)/shard_map/all_gather | solution.py:194
  166.4 5.5 %multiply_reduce_fusion = (f32[768]{0:T(1024)S(1)}, f32[768,1280]{1,0:T(8,128)S(1)}) fusion(bf16[1280,768]{1,0:T(8,128)(2,1)} %all-gather.7.cloned.1.call-done, bf16[1280,1280]{1,0:T(8,128)(2,1)} %all-gather.9.cloned.1.call-done, bf16[768,1280]{1,0:T(8,128)(2,1)S(1)} %copy-done.4), kind=kOutput, calls=%fused_computation.19 | convolution fusion | flops 2520513792 | bytes 11144192 | tf_op jit(solution)/shard_map/dot_general | solution.py:199
  172.3 2.5 reshape.285
  174.8 13.2 %convolution_convert_fusion = bf16[192,8192]{1,0:T(8,128)(2,1)} fusion(bf16[640,8192]{1,0:T(8,128)(2,1)} %param.20, bf16[192,5120]{1,0:T(8,128)(2,1)} %reshape.285, bf16[5120,640]{1,0:T(8,128)(2,1)} %param.19), kind=kOutput, calls=%fused_computation.8 | convolution fusion | flops 3281117184 | bytes 22151168 | tf_op jit(solution)/shard_map/dot_general | solution.py:220
  188.1 72.9 %reduce-scatter.2.cloned.1.call-done = bf16[24,8192]{1,0:T(8,128)(2,1)} async-done(((bf16[192,8192]{1,0:T(8,128)(2,1)}), bf16[24,8192]{1,0:T(8,128)(2,1)}) %reduce-scatter.2.cloned.1.call-update) | async-done | bytes 393232 | tf_op jit(solution)/shard_map/reduce_scatter | solution.py:219
  261.0 1.2 fusion.30
  262.2 1.9 fusion.32
  265.3 19.4 %all-gather.11.cloned.1.call-done = bf16[96,8192]{1,0:T(8,128)(2,1)} async-done(((bf16[24,8192]{1,0:T(8,128)(2,1)}), bf16[96,8192]{1,0:T(8,128)(2,1)}) %all-gather.11.cloned.1.call-update) | async-done | bytes 1572880 | tf_op jit(solution)/shard_map/all_gather | solution.py:228
  284.7 3.6 fusion.131
  288.3 4.8 %fusion.130 = f32[96,512]{1,0:T(8,128)S(1)} fusion(bf16[96,8192]{1,0:T(8,128)(2,1)S(1)} %copy-done.2, bf16[8192,512]{1,0:T(8,128)(2,1)} %param.24), kind=kOutput, calls=%fused_computation.170 | convolution fusion | flops 805306368 | bytes 10158080 | tf_op jit(solution)/shard_map/dot_general | solution.py:146
  294.9 49.5 %all-gather.15.cloned.1.call-done = bf16[512,8192]{1,0:T(8,128)(2,1)} async-done(((bf16[128,8192]{1,0:T(8,128)(2,1)}), bf16[512,8192]{1,0:T(8,128)(2,1)}) %all-gather.15.cloned.1.call-update) | async-done | bytes 8388624 | tf_op jit(solution)/shard_map/all_gather | solution.py:212
  344.4 5.3 %fusion = f32[512]{0:T(512)S(1)} fusion(bf16[512,8192]{1,0:T(8,128)(2,1)} %all-gather.15.cloned.1.call-done), kind=kLoop, calls=%fused_computation.2 | loop fusion | flops 12582400 | bytes 8390656 | tf_op jit(solution)/shard_map/reduce_sum | solution.py:22
  350.2 4.7 fusion.11
  354.9 1.2 fusion.52
  357.4 1.0 multiply_cosine_fusion.1
  358.4 1.4 fusion.4
  359.9 11.4 %fusion.13 = f32[512,512]{0,1:T(8,128)S(1)} fusion(bf16[8192,512]{1,0:T(8,128)(2,1)} %param.24, bf16[512,8192]{1,0:T(8,128)(2,1)} %all-gather.15.cloned.1.call-done, f32[8192]{0:T(1024)S(1)} %copy-done.5, f32[512]{0:T(512)S(1)} %add_rsqrt_fusion.2), kind=kOutput, calls=%fused_computation.21 | convolution fusion | flops 4311744512 | bytes 17860608 | tf_op jit(solution)/shard_map/dot_general | solution.py:146
  373.4 12.9 %all-gather.13.cloned.1.call-done = bf16[768,768]{1,0:T(8,128)(2,1)} async-done(((bf16[96,768]{1,0:T(8,128)(2,1)}), bf16[768,768]{1,0:T(8,128)(2,1)}) %all-gather.13.cloned.1.call-update) | async-done | bytes 1179664 | tf_op jit(solution)/shard_map/all_gather | solution.py:231
  386.3 2.6 fusion.27.q_ref
  388.8 47.2 %all-gather.17.cloned.1.call-done = bf16[4096,256]{1,0:T(8,128)(2,1)} async-done(((bf16[512,256]{1,0:T(8,128)(2,1)}), bf16[4096,256]{1,0:T(8,128)(2,1)}) %all-gather.17.cloned.1.call-update) | async-done | bytes 2097168 | tf_op jit(solution)/shard_map/all_gather | solution.py:217
  436.1 4.6 fusion.7
  440.7 1.5 fusion.125
  442.2 22.3 %shard_map.128 = bf16[512,512]{1,0:T(8,128)(2,1)} custom-call(s32[1]{0:T(128)} %bitcast.block_ref, bf16[512,512]{1,0:T(8,128)(2,1)} %fusion.27.q_ref, bf16[4096,128]{1,0:T(8,128)(2,1)} %get-tuple-element.10.k_ref, bf16[4096,128]{1,0:T(8,128)(2,1)} %get-tuple-element.9.v_ref), custom_call_target="tpu_custom_call" | custom-call | tf_op jit(solution)/shard_map/pallas_call | solution.py:129
  (70 shorter events, 10.7 us)
Async XLA Ops:
  6.5 5.0 %copy-start = (bf16[1280,480]{0,1:T(8,128)(2,1)S(1)}, bf16[1280,480]{0,1:T(8,128)(2,1)}, u32[]{:S(2)}) copy-start(bf16[1280,480]{0,1:T(8,128)(2,1)} %param.15) | copy-start | bytes 3686404
  6.5 97.5 %all-gather.7.cloned.1.call-start = ((), (), s32[]{:S(2)}) async-start(), calls=%async_computation.1 | async-start | bytes 2211840 | tf_op jit(solution)/shard_map/all_gather | solution.py:198
  29.0 137.4 %copy-start.4 = (bf16[768,1280]{1,0:T(8,128)(2,1)S(1)}, bf16[768,1280]{1,0:T(8,128)(2,1)}, u32[]{:S(2)}) copy-start(bf16[768,1280]{1,0:T(8,128)(2,1)} %param.13) | copy-start | bytes 5898244
  56.9 109.5 %all-gather.9.cloned.1.call-start = ((), (), s32[]{:S(2)}) async-start(), calls=%async_computation.2 | async-start | bytes 3686400 | tf_op jit(solution)/shard_map/all_gather | solution.py:194
  57.7 114.2 %copy-start.6 = (f32[1280]{0:T(1024)S(1)}, f32[1280]{0:T(1024)}, u32[]{:S(2)}) copy-start(f32[1280]{0:T(1024)} %param.18) | copy-start | bytes 15364
  57.7 203.4 %reduce-scatter.2.cloned.1.call-start = ((), (), s32[]{:S(2)}) async-start(), calls=%async_computation.3 | async-start | bytes 3538944 | tf_op jit(solution)/shard_map/reduce_scatter | solution.py:219
  174.8 87.4 %copy-start.5 = (f32[8192]{0:T(1024)S(1)}, f32[8192]{0:T(1024)}, u32[]{:S(2)}) copy-start(f32[8192]{0:T(1024)} %param.23) | copy-start | bytes 98308
  188.0 76.8 %copy-start.7 = (s32[768]{0:T(1024)S(1)}, s32[768]{0:T(1024)}, u32[]{:S(2)}) copy-start(s32[768]{0:T(1024)} %param.21) | copy-start | bytes 9220
  188.1 96.6 %all-gather.11.cloned.1.call-start = ((), (), s32[]{:S(2)}) async-start(), calls=%async_computation.4 | async-start | bytes 1966080 | tf_op jit(solution)/shard_map/all_gather | solution.py:228
  264.2 80.2 %all-gather.15.cloned.1.call-start = ((), (), s32[]{:S(2)}) async-start(), calls=%async_computation.6 | async-start | bytes 10485760 | tf_op jit(solution)/shard_map/all_gather | solution.py:212
  264.8 121.5 %all-gather.13.cloned.1.call-start = ((), (), s32[]{:S(2)}) async-start(), calls=%async_computation.5 | async-start | bytes 1327104 | tf_op jit(solution)/shard_map/all_gather | solution.py:231
  284.7 3.6 copy-start.2
  294.7 141.4 %all-gather.17.cloned.1.call-start = ((), (), s32[]{:S(2)}) async-start(), calls=%async_computation.7 | async-start | bytes 2359296 | tf_op jit(solution)/shard_map/all_gather | solution.py:217
  344.4 5.8 %copy-start.3 = (bf16[512,8192]{1,0:T(8,128)(2,1)S(1)}, bf16[512,8192]{1,0:T(8,128)(2,1)}, u32[]{:S(2)}) copy-start(bf16[512,8192]{1,0:T(8,128)(2,1)} %all-gather.15.cloned.1.call-done) | copy-start | bytes 25165828
  436.1 28.4 %copy-start.1 = (bf16[1280,480]{0,1:T(8,128)(2,1)S(1)}, bf16[1280,480]{0,1:T(8,128)(2,1)}, u32[]{:S(2)}) copy-start(bf16[1280,480]{0,1:T(8,128)(2,1)} %param.15) | copy-start | bytes 3686404
Sparse Core Ops, SparseCore 0:
  57.0 46.9 all-gather.6
  106.2 60.1 all-gather.8
  188.2 72.8 reduce-scatter.1
  264.3 20.3 all-gather.10
  286.1 58.2 all-gather.14
  346.4 39.8 all-gather.12
  388.4 47.6 all-gather.16
